TPU v7x, 32 devices: a whole 2x2x4 slice. The times are simulated.
32 devices in a mesh: groups: 2 (over y), wide: 4 (over z), narrow: 4 (over x, core).
Axes of the slice: x: 2, y: 2, z: 4, core: 2. Of those that a mesh axis runs over, the one named last changes fastest.
Arguments:
- cont_queries: bfloat16 [32, 128, 64, 128], P(('groups', 'wide'), None, 'narrow'), parts along dimension 0, may hold values from -5 to 5
- cont_keys: bfloat16 [32, 128, 8, 128], P(('groups', 'wide'), None, 'narrow'), parts along dimension 0, may hold values from -5 to 5
- cont_values: bfloat16 [32, 128, 8, 128], P(('groups', 'wide'), None, 'narrow'), parts along dimension 0, may hold values from -5 to 5
- prefix_kv: bfloat16 [8, 2, 128, 8, 128], P(('groups', 'wide'), None, None, 'narrow'), parts along dimension 0, may hold values from -5 to 5
- probe: bfloat16 [64, 128], P('narrow'), may hold values from -0.5 to 0.5
- question_row: int32 [8], P('groups'), parts along dimension 0, may hold values from 0 to 3, each once
- cont_slot: int32 [32], P(('groups', 'wide')), parts along dimension 0, may hold values from 0 to 15, each once
- cont_length: int32 [32], P(('groups', 'wide')), parts along dimension 0, may hold values from 1 to 128
- gold: int32 [8], P('groups'), parts along dimension 0, may hold values from 0 to 3
Outputs:
- token_score: float32 [32, 128], P(('groups', 'wide')), parts along dimension 0
- owned_logprob: float32 [8, 4], P(('groups', 'wide')), parts along dimension 0
- owned_loss: float32 [8], P(('groups', 'wide')), parts along dimension 0
There are 2 independent parts, one for each index of `groups`. A program takes and returns all parts, laid end to end along the dimension named above; an argument that names none is the same for every part. Nothing has to cross between parts.
All inputs are finite; a program needn't handle non-finite values.
Results may differ from a plain program's by a relative error of at most 0.0065.
Values may be sent and summed in bfloat16 or wider, within the bound.
A program may use at most 64 MiB of HBM per device.

v0:
```python
import functools

import jax
import jax.numpy as jnp
from jax import lax
from jax.experimental import pallas as pl
from jax.experimental.pallas import tpu as pltpu
from jax.sharding import PartitionSpec as P

MESH = pl.DeviceIdType.MESH
ANSWERS = 4
LANES = 128
NEG = -1e30
LOG2E = 1.4426950408889634
F32 = jnp.float32
BF16 = jnp.bfloat16
NT = (((1,), (1,)), ((), ()))
TN = (((0,), (0,)), ((), ()))


def iota(shape, dim):
    return lax.broadcasted_iota(jnp.int32, shape, dim)


def kernel(
    sizes,
    qrow_hbm, slot_hbm, len_hbm, gold_hbm, q_hbm, k_hbm, v_hbm, pre_hbm, probe_hbm,
    out_ref,
    qrow_ref, slot_ref, len_ref, gold_ref, probe_ref, q2_v,
    q_v, k_v, v_v, pv_v, kslot, vpslot, split, kown, vpt, kpre, vptp,
    m1, l1, n1, m2, l2, n2, tslot, cbuf, cslot,
    in_sem, ksend, krecv, vsend, vrecv, tsend, trecv, csend, crecv,
):
    wide, narrow, conts, clen, heads, kv, dim, quest, pref, questions = sizes
    group = heads // kv
    scale = LOG2E / dim**0.5
    me_w = lax.axis_index("wide")
    me_n = lax.axis_index("narrow")
    tcols = 2 * LANES // heads
    cols = tcols * heads
    blocks = clen // tcols
    own = pl.ds(me_w * quest, quest)

    cp_k = pltpu.make_async_copy(pre_hbm.at[:, 0], kslot.at[own], in_sem.at[0])
    cp_v = pltpu.make_async_copy(pre_hbm.at[:, 1], pv_v, in_sem.at[1])
    cp_ko = pltpu.make_async_copy(k_hbm, k_v, in_sem.at[2])
    cp_vo = pltpu.make_async_copy(v_hbm, v_v, in_sem.at[3])
    cp_q = pltpu.make_async_copy(q_hbm, q_v, in_sem.at[4])
    cp_p = pltpu.make_async_copy(probe_hbm, probe_ref, in_sem.at[5])
    scalars = [
        pltpu.make_async_copy(src, dst, in_sem.at[6 + i])
        for i, (src, dst) in enumerate(
            ((qrow_hbm, qrow_ref), (slot_hbm, slot_ref), (len_hbm, len_ref), (gold_hbm, gold_ref))
        )
    ]
    for cp in (cp_k, cp_v, cp_p, cp_ko, cp_vo, cp_q, *scalars):
        cp.start()

    total = wide * narrow
    me = me_w * narrow + me_n
    right, left = lax.rem(me_w + 1, wide), lax.rem(me_w + wide - 1, wide)

    def peer(i):
        p = lax.rem(me + i, total)
        return {"wide": lax.div(p, narrow), "narrow": lax.rem(p, narrow)}

    barrier = pltpu.get_barrier_semaphore()
    near = [{"wide": right}, {"wide": left}]
    near += [{"narrow": lax.rem(me_n + i, narrow)} for i in range(1, narrow)]
    for to in near:
        pl.semaphore_signal(barrier, inc=1, device_id=to, device_id_type=MESH)

    pl.semaphore_wait(barrier, len(near))

    steps = wide // 2

    def ring_copy(buf, sends, recvs, step, way, half):
        size = buf.shape[1] // 2
        row = lax.rem(me_w + (wide - step + 1 if way == 0 else step - 1), wide)
        part = buf.at[pl.ds(row * quest, quest), pl.ds(half * size, size)]
        n = ((step - 1) * 2 + way) * 2 + half
        return pltpu.make_async_remote_copy(
            src_ref=part, dst_ref=part, send_sem=sends.at[n], recv_sem=recvs.at[n],
            device_id={"wide": right if way == 0 else left}, device_id_type=MESH,
        )

    def ring_step(step):
        out = []
        for turn in range(2 if step < steps else 1):
            for way in range(2):
                half = way if turn == 0 else 1 - way
                for args in ((vpslot, vsend, vrecv), (kslot, ksend, krecv)):
                    out.append(ring_copy(*args, step, way, half))
        return out

    pending = ring_step(1)
    first_k, first_v, rest_k, rest_v = pending[1:4:2], pending[0:4:2], pending[5::2], pending[4::2]
    cp_k.wait()
    for cp in first_k:
        cp.start()

    cp_p.wait()
    probe = probe_ref[...]
    lane = iota((1, LANES), 1)
    lane_kv = (lane % heads) // group
    rowsel = iota((LANES, heads), 0) % heads == iota((LANES, heads), 1)
    tile_mat = jnp.where(rowsel, 1.0, 0.0).astype(BF16)
    probe_t = lax.dot_general(
        tile_mat, probe, (((1,), (0,)), ((), ())), preferred_element_type=F32
    ).astype(BF16)
    expand = jnp.where(iota((heads, LANES), 1) % heads == iota((heads, LANES), 0), 1.0, 0.0)

    def unpack(x):
        split[...] = x.astype(F32)
        n = x.shape[0] // kv
        return [split[pl.ds(i, n, stride=kv), :] for i in range(kv)]

    cp_v.wait()
    head_kv = iota((heads, 1), 0) // group
    for r in range(quest):
        acc = jnp.zeros((heads, pref), F32)
        for i, part in enumerate(unpack(pv_v[r])):
            d = lax.dot_general(probe, part.astype(BF16), NT, preferred_element_type=F32)
            acc = jnp.where(head_kv == i, d, acc)
        vpslot[me_w * quest + r] = acc
    for cp in (*first_v, *rest_v, *rest_k):
        cp.start()

    def each_peer(count, fn):
        def step(i, _):
            fn(i)
            return 0
        lax.fori_loop(1, count, step, 0)

    def start_mask(c, b):
        rows = q_v[c, pl.ds(b * cols, cols), :]
        rk = (iota((cols, 1), 0) % heads) // group
        return jnp.concatenate(
            [rows * jnp.where(rk == i, 1.0, 0.0).astype(BF16) for i in range(kv)], axis=1
        )

    def softmax_part(s, vp):
        m = jnp.max(s, axis=0, keepdims=True)
        e = jnp.exp2((s - m) * scale)
        l = jnp.sum(e, axis=0, keepdims=True)
        n = jnp.sum(e * jnp.concatenate([vp] * (cols // LANES), axis=1), axis=0, keepdims=True)
        return m, l, n

    cp_ko.wait()
    cp_vo.wait()
    cp_q.wait()
    block_id = iota((blocks, cols), 0)

    def gather(stats, b, news):
        return [jnp.where(block_id == b, new, old) for new, old in zip(news, stats)]

    blank = jnp.zeros((blocks, cols), F32)

    def own_part(c, _):
        parts = unpack(k_v[c])
        for i in range(kv):
            kown[:, i * dim:(i + 1) * dim] = parts[i].astype(BF16)
        d = lax.dot_general(v_v[c], probe_t, NT, preferred_element_type=F32)
        split[...] = d
        acc = split[pl.ds(0, clen, stride=kv), :]
        for i in range(1, kv):
            acc = jnp.where(lane_kv == i, split[pl.ds(i, clen, stride=kv), :], acc)
        vpt[...] = acc
        stats = [blank] * 3
        for b in range(blocks):
            n_rows = (b + 1) * tcols
            q2 = start_mask(c, b)
            q2_v[c, pl.ds(b * cols, cols), :] = q2
            s = lax.dot_general(kown[:n_rows, :], q2, NT, preferred_element_type=F32)
            ok = iota((tcols, cols), 0) <= iota((tcols, cols), 1) // heads
            last = jnp.where(ok, s[n_rows - tcols:], NEG)
            s = last if b == 0 else jnp.concatenate([s[:n_rows - tcols], last], axis=0)
            m, l, n = softmax_part(s, vpt[:n_rows, :])
            stats = gather(stats, b, (m, l, n))
        m1[c], l1[c], n1[c] = stats
        return 0

    lax.fori_loop(0, conts, own_part, 0)

    sent = list(pending)
    for step in range(2, steps + 1):
        later = ring_step(step)
        lead = len(later) if step == steps else 0
        for got, cp in zip(pending[:lead], later[:lead]):
            got.wait_recv()
            cp.start()
        for got in pending[lead:]:
            got.wait_recv()
        if lead == 0:
            for cp in later:
                cp.start()
        sent += later
        pending = later
    for cp in pending:
        cp.wait_recv()
    for cp in sent:
        cp.wait_send()

    for cp in scalars:
        cp.wait()

    def prefix_part(c, _):
        w = qrow_ref[slot_ref[c] // ANSWERS]
        parts = unpack(kslot[w])
        for i in range(kv):
            kpre[:, i * dim:(i + 1) * dim] = parts[i].astype(BF16)
        vptp[...] = lax.dot_general(
            vpslot[w], expand, TN, preferred_element_type=F32, precision=lax.Precision.HIGHEST
        )
        stats = [blank] * 3
        for b in range(blocks):
            q2 = q2_v[c, pl.ds(b * cols, cols), :]
            s = lax.dot_general(kpre[...], q2, NT, preferred_element_type=F32)
            m, l, n = softmax_part(s, vptp[...])
            stats = gather(stats, b, (m, l, n))
        m2[c], l2[c], n2[c] = stats
        return 0

    lax.fori_loop(0, conts, prefix_part, 0)

    fold = jnp.where(iota((cols, clen), 0) // heads == iota((cols, clen), 1) % tcols, 1.0, 0.0)
    keep = iota((blocks, clen), 1) // tcols == iota((blocks, clen), 0)
    row_id = iota((conts, clen), 0)
    partial = jnp.zeros((conts, clen), F32)
    for c in range(conts):
        ma, mb = m1[c], m2[c]
        m = jnp.maximum(ma, mb)
        ea, eb = jnp.exp2((ma - m) * scale), jnp.exp2((mb - m) * scale)
        ratio = (n1[c] * ea + n2[c] * eb) / (l1[c] * ea + l2[c] * eb)
        y = jnp.dot(ratio, fold, preferred_element_type=F32, precision=lax.Precision.HIGHEST)
        y = jnp.sum(jnp.where(keep, y, 0.0), axis=0, keepdims=True)
        partial = jnp.where(row_id == c, y, partial)
    tslot[me_n] = partial

    choice_rows = wide * quest
    crow = iota((wide, quest, LANES), 0) * quest + iota((wide, quest, LANES), 1)
    clane = iota((wide, quest, LANES), 2)
    term = jnp.zeros((wide, quest, LANES), F32)
    tpos = iota((1, clen), 1)
    for c in range(conts):
        slot = slot_ref[c]
        w = qrow_ref[slot // ANSWERS]
        a = slot % ANSWERS
        val = jnp.sum(jnp.where(tpos < len_ref[c], partial[c:c + 1, :], 0.0), axis=1, keepdims=True)
        term = term + jnp.where((crow == w) & (clane == a), val.reshape(1, 1, 1), 0.0)
    cbuf[...] = term

    def tcopy(i):
        return pltpu.make_async_remote_copy(
            src_ref=tslot.at[me_n], dst_ref=tslot.at[me_n],
            send_sem=tsend.at[i - 1], recv_sem=trecv.at[i - 1],
            device_id={"narrow": lax.rem(me_n + i, narrow)}, device_id_type=MESH,
        )

    def ccopy(i):
        to = peer(i)
        return pltpu.make_async_remote_copy(
            src_ref=cbuf.at[to["wide"]], dst_ref=cslot.at[me],
            send_sem=csend.at[i - 1], recv_sem=crecv.at[i - 1],
            device_id=to, device_id_type=MESH,
        )

    each_peer(total, lambda i: ccopy(i).start())
    each_peer(narrow, lambda i: tcopy(i).start())
    cslot[me] = cbuf[me_w]

    each_peer(narrow, lambda i: tcopy(i).wait())
    tok = tslot[0]
    for i in range(1, narrow):
        tok = tok + tslot[i]
    out_ref[0:conts, :] = tok

    each_peer(total, lambda i: ccopy(i).wait())
    scores = jnp.sum(cslot[...], axis=0)
    live = iota((quest, LANES), 1) < ANSWERS
    masked = jnp.where(live, scores, NEG)
    top = jnp.max(masked, axis=1, keepdims=True)
    norm = jnp.log(jnp.sum(jnp.where(live, jnp.exp(masked - top), 0.0), axis=1, keepdims=True))
    logp = scores - top - norm
    out_ref[conts:conts + quest, :] = logp
    mine = me_w * quest + iota((quest, 1), 0)
    gold = jnp.zeros((quest, 1), jnp.int32)
    for g in range(questions):
        gold = jnp.where(mine == qrow_ref[g], gold_ref[g], gold)
    pick = iota((quest, LANES), 1) == gold
    loss = -jnp.sum(jnp.where(pick, logp, 0.0), axis=1, keepdims=True)
    out_ref[conts + quest:conts + 2 * quest, :] = jnp.broadcast_to(loss, (quest, LANES))


def hand_out(conts, quest, packed_ref, tok_ref, logp_ref, loss_ref):
    tok_ref[...] = packed_ref[0:conts, :]
    logp_ref[...] = packed_ref[conts:conts + quest, :ANSWERS]
    loss_ref[...] = packed_ref[conts + quest:conts + 2 * quest, :1]


def solution(mesh):
    wide, narrow = mesh.shape["wide"], mesh.shape["narrow"]
    total = wide * narrow

    def per_device(q, k, v, prefix, probe, qrow, slot, length, gold):
        conts, clen, heads, dim = q.shape
        kv = k.shape[2]
        quest, _, pref = prefix.shape[:3]
        questions = qrow.shape[0]
        cols = 2 * LANES // heads * heads
        blocks = clen * heads // cols
        sizes = (wide, narrow, conts, clen, heads, kv, dim, quest, pref, questions)
        vmem = pl.BlockSpec(memory_space=pltpu.VMEM)
        anyw = pl.BlockSpec(memory_space=pl.ANY)
        stat = pltpu.VMEM((conts, blocks, cols), F32)
        dma = pltpu.SemaphoreType.DMA
        packed = pl.pallas_call(
            functools.partial(kernel, sizes),
            out_shape=jax.ShapeDtypeStruct((conts + 2 * quest, LANES), F32),
            in_specs=[anyw] * 9,
            out_specs=vmem,
            scratch_shapes=[
                pltpu.SMEM((questions,), jnp.int32),
                pltpu.SMEM((conts,), jnp.int32),
                pltpu.SMEM((conts,), jnp.int32),
                pltpu.SMEM((questions,), jnp.int32),
                pltpu.VMEM((heads, dim), BF16),
                pltpu.VMEM((conts, clen * heads, kv * dim), BF16),
                pltpu.VMEM((conts, clen * heads, dim), BF16),
                pltpu.VMEM((conts, clen * kv, dim), BF16),
                pltpu.VMEM((conts, clen * kv, dim), BF16),
                pltpu.VMEM((quest, pref * kv, dim), BF16),
                pltpu.VMEM((wide * quest, pref * kv, dim), BF16),
                pltpu.VMEM((wide * quest, heads, pref), F32),
                pltpu.VMEM((clen * kv, dim), F32),
                pltpu.VMEM((clen, kv * dim), BF16),
                pltpu.VMEM((clen, LANES), F32),
                pltpu.VMEM((pref, kv * dim), BF16),
                pltpu.VMEM((pref, LANES), F32),
                stat, stat, stat, stat, stat, stat,
                pltpu.VMEM((narrow, conts, clen), F32),
                pltpu.VMEM((wide, quest, LANES), F32),
                pltpu.VMEM((total, quest, LANES), F32),
                dma((10,)),
                dma((2 * wide,)), dma((2 * wide,)), dma((2 * wide,)), dma((2 * wide,)),
                dma((narrow - 1,)), dma((narrow - 1,)), dma((total - 1,)), dma((total - 1,)),
            ],
            compiler_params=pltpu.CompilerParams(collective_id=0, has_side_effects=True),
        )(
            qrow, slot, length, gold,
            q.reshape(conts, clen * heads, dim),
            k.reshape(conts, clen * kv, dim),
            v.reshape(conts, clen * kv, dim),
            prefix.reshape(quest, 2, pref * kv, dim),
            probe,
        )
        tok, logp, loss = pl.pallas_call(
            functools.partial(hand_out, conts, quest),
            out_shape=(
                jax.ShapeDtypeStruct((conts, clen), F32),
                jax.ShapeDtypeStruct((quest, ANSWERS), F32),
                jax.ShapeDtypeStruct((quest, 1), F32),
            ),
            in_specs=[vmem],
            out_specs=(vmem, vmem, vmem),
        )(packed)
        return tok, logp, loss.reshape(quest)

    return jax.shard_map(
        per_device,
        mesh=mesh,
        in_specs=(
            P(("groups", "wide"), None, "narrow", None),
            P(("groups", "wide"), None, "narrow", None),
            P(("groups", "wide"), None, "narrow", None),
            P(("groups", "wide"), None, None, "narrow", None),
            P("narrow", None),
            P("groups"),
            P(("groups", "wide")),
            P(("groups", "wide")),
            P("groups"),
        ),
        out_specs=(P(("groups", "wide"), None), P(("groups", "wide"), None), P(("groups", "wide"))),
        check_vma=False,
    )
```

profile of v0, /device:TPU:0, one launch (start us, length us, event | category | flops | bytes accessed | tf_op | source)
XLA Modules:
  0.0 24.2 jit_solution(11950296930038442194)
XLA Ops:
  0.6 22.3 %shard_map.112.packed_ref = f32[6,128]{1,0:T(8,128)} custom-call(s32[4]{0:T(128)} %qrow_hbm.1, s32[4]{0:T(128)} %slot_hbm.1, s32[4]{0:T(128)} %len_hbm.1, s32[4]{0:T(128)} %gold_hbm.1, bf16[4,2048,128]{2,1,0:T(8,128)(2,1)} %bitcast.5, bf16[4,256,128]{2,1,0:T(8,128)(2,1)} %bitcast.6, bf16[4,256,128]{2,1,0:T(8,128)(2,1)} %bitcast.7, ...), custom_call_target="tpu_custom_call" | custom-call | tf_op jit(solution)/shard_map/pallas_call | solution.py:317
  23.0 1.3 %shard_map.113 = (f32[4,128]{1,0:T(4,128)}, f32[1,4]{1,0:T(1,128)}, f32[1,1]{1,0:T(1,128)}) custom-call(f32[6,128]{1,0:T(8,128)} %shard_map.112.packed_ref), custom_call_target="tpu_custom_call" | custom-call | tf_op jit(solution)/shard_map/pallas_call | solution.py:357
where the time goes:
time: 24.4 us; the launch traced here: 24.2 us
  Pallas kernels  23.6 us (97%)
  between operations  0.64 us (3%)
    pallas_call x1, Pallas kernels, per_device(): pl.pallas_call(functools.partial(kernel, sizes), out_shape=jax.ShapeDtype...  22.3 us
    pallas_call x1, Pallas kernels, per_device(): pl.pallas_call(functools.partial(hand_out, conts, quest), out_shape=(jax....  1.26 us

commit v1 on v0

--- a/solution.py
+++ b/solution.py
@@ -29,7 +29,7 @@
     qrow_ref, slot_ref, len_ref, gold_ref, probe_ref, q2_v,
     q_v, k_v, v_v, pv_v, kslot, vpslot, split, kown, vpt, kpre, vptp,
     m1, l1, n1, m2, l2, n2, tslot, cbuf, cslot,
-    in_sem, ksend, krecv, vsend, vrecv, tsend, trecv, csend, crecv,
+    in_sem, send_sem, recv_sem,
 ):
     wide, narrow, conts, clen, heads, kv, dim, quest, pref, questions = sizes
     group = heads // kv
@@ -58,46 +58,32 @@
 
     total = wide * narrow
     me = me_w * narrow + me_n
-    right, left = lax.rem(me_w + 1, wide), lax.rem(me_w + wide - 1, wide)
-
-    def peer(i):
-        p = lax.rem(me + i, total)
-        return {"wide": lax.div(p, narrow), "narrow": lax.rem(p, narrow)}
+    far = sorted(range(1, wide), key=lambda i: (-min(i, wide - i), i))
+    wides = [lax.rem(me_w + i, wide) for i in range(wide)]
+    narrows = [lax.rem(me_n + i, narrow) for i in range(narrow)]
 
     barrier = pltpu.get_barrier_semaphore()
-    near = [{"wide": right}, {"wide": left}]
-    near += [{"narrow": lax.rem(me_n + i, narrow)} for i in range(1, narrow)]
+    near = [{"wide": wides[i]} for i in far] + [{"narrow": to} for to in narrows[1:]]
     for to in near:
         pl.semaphore_signal(barrier, inc=1, device_id=to, device_id_type=MESH)
-
     pl.semaphore_wait(barrier, len(near))
 
-    steps = wide // 2
-
-    def ring_copy(buf, sends, recvs, step, way, half):
-        size = buf.shape[1] // 2
-        row = lax.rem(me_w + (wide - step + 1 if way == 0 else step - 1), wide)
-        part = buf.at[pl.ds(row * quest, quest), pl.ds(half * size, size)]
-        n = ((step - 1) * 2 + way) * 2 + half
+    def remote(src, dst, n, to):
         return pltpu.make_async_remote_copy(
-            src_ref=part, dst_ref=part, send_sem=sends.at[n], recv_sem=recvs.at[n],
-            device_id={"wide": right if way == 0 else left}, device_id_type=MESH,
-        )
-
-    def ring_step(step):
-        out = []
-        for turn in range(2 if step < steps else 1):
-            for way in range(2):
-                half = way if turn == 0 else 1 - way
-                for args in ((vpslot, vsend, vrecv), (kslot, ksend, krecv)):
-                    out.append(ring_copy(*args, step, way, half))
-        return out
-
-    pending = ring_step(1)
-    first_k, first_v, rest_k, rest_v = pending[1:4:2], pending[0:4:2], pending[5::2], pending[4::2]
+            src_ref=src, dst_ref=dst, send_sem=send_sem.at[n], recv_sem=recv_sem.at[n],
+            device_id=to, device_id_type=MESH,
+        )
+
+    def share(buf, n):
+        for i in far:
+            remote(buf.at[own], buf.at[own], n, {"wide": wides[i]}).start()
+
+    def drained(buf, n, count):
+        part = buf.at[pl.ds(0, count)]
+        return remote(part, part, n, {"wide": wides[1]})
+
     cp_k.wait()
-    for cp in first_k:
-        cp.start()
+    share(kslot, 0)
 
     cp_p.wait()
     probe = probe_ref[...]
@@ -123,14 +109,7 @@
             d = lax.dot_general(probe, part.astype(BF16), NT, preferred_element_type=F32)
             acc = jnp.where(head_kv == i, d, acc)
         vpslot[me_w * quest + r] = acc
-    for cp in (*first_v, *rest_v, *rest_k):
-        cp.start()
-
-    def each_peer(count, fn):
-        def step(i, _):
-            fn(i)
-            return 0
-        lax.fori_loop(1, count, step, 0)
+    share(vpslot, 1)
 
     def start_mask(c, b):
         rows = q_v[c, pl.ds(b * cols, cols), :]
@@ -182,24 +161,10 @@
 
     lax.fori_loop(0, conts, own_part, 0)
 
-    sent = list(pending)
-    for step in range(2, steps + 1):
-        later = ring_step(step)
-        lead = len(later) if step == steps else 0
-        for got, cp in zip(pending[:lead], later[:lead]):
-            got.wait_recv()
-            cp.start()
-        for got in pending[lead:]:
-            got.wait_recv()
-        if lead == 0:
-            for cp in later:
-                cp.start()
-        sent += later
-        pending = later
-    for cp in pending:
-        cp.wait_recv()
-    for cp in sent:
-        cp.wait_send()
+    others = (wide - 1) * quest
+    for n, buf in ((0, kslot), (1, vpslot)):
+        drained(buf, n, others).wait_recv()
+        drained(buf, n, others).wait_send()
 
     for cp in scalars:
         cp.wait()
@@ -250,32 +215,35 @@
         term = term + jnp.where((crow == w) & (clane == a), val.reshape(1, 1, 1), 0.0)
     cbuf[...] = term
 
-    def tcopy(i):
-        return pltpu.make_async_remote_copy(
-            src_ref=tslot.at[me_n], dst_ref=tslot.at[me_n],
-            send_sem=tsend.at[i - 1], recv_sem=trecv.at[i - 1],
-            device_id={"narrow": lax.rem(me_n + i, narrow)}, device_id_type=MESH,
-        )
-
-    def ccopy(i):
-        to = peer(i)
-        return pltpu.make_async_remote_copy(
-            src_ref=cbuf.at[to["wide"]], dst_ref=cslot.at[me],
-            send_sem=csend.at[i - 1], recv_sem=crecv.at[i - 1],
-            device_id=to, device_id_type=MESH,
-        )
-
-    each_peer(total, lambda i: ccopy(i).start())
-    each_peer(narrow, lambda i: tcopy(i).start())
+    def hand(i, j):
+        to = {"wide": wides[i], "narrow": narrows[j]}
+        remote(cbuf.at[wides[i]], cslot.at[me], 2, to).start()
+
+    if total <= 16:
+        for j in range(narrow - 1, -1, -1):
+            for i in (*far, 0):
+                if i or j:
+                    hand(i, j)
+    else:
+        @pl.loop(1, total)
+        def _(n):
+            p = lax.rem(me + n, total)
+            to = {"wide": lax.div(p, narrow), "narrow": lax.rem(p, narrow)}
+            remote(cbuf.at[to["wide"]], cslot.at[me], 2, to).start()
+
+    for j in range(1, narrow):
+        remote(tslot.at[me_n], tslot.at[me_n], 3, {"narrow": narrows[j]}).start()
     cslot[me] = cbuf[me_w]
 
-    each_peer(narrow, lambda i: tcopy(i).wait())
+    drained(tslot, 3, narrow - 1).wait_recv()
     tok = tslot[0]
     for i in range(1, narrow):
         tok = tok + tslot[i]
     out_ref[0:conts, :] = tok
 
-    each_peer(total, lambda i: ccopy(i).wait())
+    drained(cslot, 2, total - 1).wait_recv()
+    drained(tslot, 3, narrow - 1).wait_send()
+    drained(cslot, 2, total - 1).wait_send()
     scores = jnp.sum(cslot[...], axis=0)
     live = iota((quest, LANES), 1) < ANSWERS
     masked = jnp.where(live, scores, NEG)
@@ -316,7 +284,7 @@
         dma = pltpu.SemaphoreType.DMA
         packed = pl.pallas_call(
             functools.partial(kernel, sizes),
-            out_shape=jax.ShapeDtypeStruct((conts + 2 * quest, LANES), F32),
+            out_shape=pltpu.VMEM((conts + 2 * quest, LANES), F32),
             in_specs=[anyw] * 9,
             out_specs=vmem,
             scratch_shapes=[
@@ -342,8 +310,7 @@
                 pltpu.VMEM((wide, quest, LANES), F32),
                 pltpu.VMEM((total, quest, LANES), F32),
                 dma((10,)),
-                dma((2 * wide,)), dma((2 * wide,)), dma((2 * wide,)), dma((2 * wide,)),
-                dma((narrow - 1,)), dma((narrow - 1,)), dma((total - 1,)), dma((total - 1,)),
+                dma((4,)), dma((4,)),
             ],
             compiler_params=pltpu.CompilerParams(collective_id=0, has_side_effects=True),
         )(
@@ -363,7 +330,7 @@
             ),
             in_specs=[vmem],
             out_specs=(vmem, vmem, vmem),
-        )(packed)
+        )(pltpu.with_memory_space_constraint(packed, pltpu.VMEM))
         return tok, logp, loss.reshape(quest)
 
     return jax.shard_map(

time: 24.4 us -> 22.1 us (0.906)
  Pallas kernels: 23.6 us -> 21.3 us
    pallas_call x1, Pallas kernels: 22.3 us -> 20.7 us  [per_device(): pl.pallas_call(functools.partial(kernel, sizes), out_shape=pltpu.VMEM((co...]
    pallas_call x1, Pallas kernels: 1.26 us -> 0.59 us  [per_device(): pl.pallas_call(functools.partial(hand_out, conts, quest), out_shape=(jax....]
where the time goes in v1:
time: 22.1 us; the launch traced here: 21.9 us
  Pallas kernels  21.3 us (96%)
  between operations  0.64 us (3%)
    pallas_call x1, Pallas kernels, per_device(): pl.pallas_call(functools.partial(kernel, sizes), out_shape=pltpu.VMEM((co...  20.7 us
    pallas_call x1, Pallas kernels, per_device(): pl.pallas_call(functools.partial(hand_out, conts, quest), out_shape=(jax....  0.59 us

profile of v1, /device:TPU:0, one launch (start us, length us, event | category | flops | bytes accessed | tf_op | source)
XLA Modules:
  0.0 21.9 jit_solution(9396754897210158898)
XLA Ops:
  0.6 20.7 %shard_map.112.packed_ref = f32[6,128]{1,0:T(8,128)S(1)} custom-call(s32[4]{0:T(128)} %qrow_hbm.1, s32[4]{0:T(128)} %slot_hbm.1, s32[4]{0:T(128)} %len_hbm.1, s32[4]{0:T(128)} %gold_hbm.1, bf16[4,2048,128]{2,1,0:T(8,128)(2,1)} %bitcast.5, bf16[4,256,128]{2,1,0:T(8,128)(2,1)} %bitcast.6, bf16[4,256,128]{2,1,0:T(8,128)(2,1)} %bitcast.7, ...), custom_call_target="tpu_custom_call" | custom-call | tf_op jit(solution)/shard_map/pallas_call | solution.py:285
  21.4 0.6 %shard_map.113 = (f32[4,128]{1,0:T(4,128)}, f32[1,4]{1,0:T(1,128)}, f32[1,1]{1,0:T(1,128)}) custom-call(f32[6,128]{1,0:T(8,128)S(1)} %shard_map.112.packed_ref), custom_call_target="tpu_custom_call" | custom-call | tf_op jit(solution)/shard_map/pallas_call | solution.py:324

commit v2 on v1

v2 whole, which is shorter than its diff:
```python
import functools

import jax
import jax.numpy as jnp
from jax import lax
from jax.experimental import pallas as pl
from jax.experimental.pallas import tpu as pltpu
from jax.sharding import PartitionSpec as P

MESH = pl.DeviceIdType.MESH
ANSWERS = 4
LANES = 128
SUBLANES = 8
NEG = -1e30
LOG2E = 1.4426950408889634
F32 = jnp.float32
BF16 = jnp.bfloat16
NT = (((1,), (1,)), ((), ()))
TN = (((0,), (0,)), ((), ()))


def iota(shape, dim):
    return lax.broadcasted_iota(jnp.int32, shape, dim)


def kernel(
    sizes,
    qrow_hbm, slot_hbm, len_hbm, gold_hbm, q_hbm, k_hbm, v_hbm, pre_hbm, probe_hbm,
    out_ref,
    qrow_ref, slot_ref, len_ref, gold_ref, probe_ref, qt_v,
    q_v, k_v, v_v, pv_v, kslot_a, kslot_b, vpslot, split, kown, vpt, kpre, vptp,
    ms, ls, ns, tslot, cbuf, cslot,
    in_sem, send_sem, recv_sem, ready, column, everyone,
):
    wide, narrow, conts, clen, heads, kv, dim, quest, pref, questions = sizes
    group = heads // kv
    scale = LOG2E / dim**0.5
    me_w = lax.axis_index("wide")
    me_n = lax.axis_index("narrow")
    tcols = 2 * LANES // heads
    cols = tcols * heads
    blocks = clen // tcols
    own = pl.ds(me_w * quest, quest)

    half = pref // 2
    kslots = (kslot_a, kslot_b)
    cp_ks = [
        pltpu.make_async_copy(
            pre_hbm.at[:, 0, pl.ds(i * half * kv, half * kv)], ref.at[own], in_sem.at[10 * i]
        )
        for i, ref in enumerate(kslots)
    ]
    cp_v = pltpu.make_async_copy(pre_hbm.at[:, 1], pv_v, in_sem.at[1])
    cp_ko = pltpu.make_async_copy(k_hbm, k_v, in_sem.at[2])
    cp_vo = pltpu.make_async_copy(v_hbm, v_v, in_sem.at[3])
    cp_q = pltpu.make_async_copy(q_hbm, q_v, in_sem.at[4])
    cp_p = pltpu.make_async_copy(probe_hbm, probe_ref, in_sem.at[5])
    scalars = [
        pltpu.make_async_copy(src, dst, in_sem.at[6 + i])
        for i, (src, dst) in enumerate(
            ((qrow_hbm, qrow_ref), (slot_hbm, slot_ref), (len_hbm, len_ref), (gold_hbm, gold_ref))
        )
    ]
    for cp in (*cp_ks, cp_v, cp_p, cp_ko, cp_vo, cp_q, *scalars):
        cp.start()

    total = wide * narrow
    me = me_w * narrow + me_n
    far = sorted(range(1, wide), key=lambda i: (-min(i, wide - i), i))
    wides = [lax.rem(me_w + i, wide) for i in range(wide)]
    narrows = [lax.rem(me_n + i, narrow) for i in range(narrow)]
    first = me_w == 0
    patient = first | (lax.rem(me_n, 2) == 1)

    def signal(sem, to):
        pl.semaphore_signal(sem, inc=1, device_id=to, device_id_type=MESH)

    def each(low, high, fn):
        def step(i, _):
            fn(i)
            return 0
        lax.fori_loop(low, high, step, 0)

    def earlier(fn):
        each(0, me_w, fn)

    def later(fn):
        each(me_w + 1, wide, fn)

    barrier = pltpu.get_barrier_semaphore()
    later(lambda p: signal(barrier, {"wide": p}))

    @pl.when(first)
    def _():
        for to in narrows[1:]:
            signal(barrier, {"narrow": to})

    pl.semaphore_wait(barrier, jnp.where(first, narrow - 1, me_w))
    earlier(lambda p: signal(ready.at[me_w], {"wide": p}))

    def remote(src, dst, n, to):
        return pltpu.make_async_remote_copy(
            src_ref=src, dst_ref=dst, send_sem=send_sem.at[n], recv_sem=recv_sem.at[n],
            device_id=to, device_id_type=MESH,
        )

    def share(buf, n):
        return lambda p: remote(buf.at[own], buf.at[own], n, {"wide": p}).start()

    def drained(buf, n, count):
        part = buf.at[pl.ds(0, count)]
        return remote(part, part, n, {"wide": wides[1]})

    cp_ks[0].wait()
    earlier(share(kslot_a, 0))

    cp_p.wait()
    probe = probe_ref[...]
    lane = iota((1, LANES), 1)
    lane_kv = (lane % heads) // group
    rowsel = iota((LANES, heads), 0) % heads == iota((LANES, heads), 1)
    tile_mat = jnp.where(rowsel, 1.0, 0.0).astype(BF16)
    probe_t = lax.dot_general(
        tile_mat, probe, (((1,), (0,)), ((), ())), preferred_element_type=F32
    ).astype(BF16)
    expand = jnp.where(iota((heads, LANES), 1) % heads == iota((heads, LANES), 0), 1.0, 0.0).astype(BF16)

    def unpack(x):
        n = x.shape[0] // kv
        split[0:n * kv] = x.astype(F32)
        return [split[pl.ds(i, n, stride=kv), :] for i in range(kv)]

    cp_v.wait()
    head_kv = iota((heads, 1), 0) // group
    for r in range(quest):
        acc = jnp.zeros((heads, pref), F32)
        for i, part in enumerate(unpack(pv_v[r])):
            d = lax.dot_general(probe, part.astype(BF16), NT, preferred_element_type=F32)
            acc = jnp.where(head_kv == i, d, acc)
        vpslot[me_w * quest + r] = acc.astype(BF16)
    earlier(share(vpslot, 1))

    def meet(p):
        pl.semaphore_wait(ready.at[p], 1)
        share(kslot_a, 0)(p)
        share(vpslot, 1)(p)

    later(meet)
    cp_ks[1].wait()

    def share_rest():
        later(share(kslot_b, 4))
        earlier(share(kslot_b, 4))

    @pl.when(jnp.logical_not(patient))
    def _():
        share_rest()

    @pl.when(first)
    def _():
        for to in narrows[1:]:
            signal(column, {"narrow": to})


    lane_q = (iota((1, cols), 1) % heads) // group
    q_masks = [jnp.where(lane_q == i, 1.0, 0.0).astype(BF16) for i in range(kv)]

    def turn(c, b):
        rows = q_v[c, pl.ds(b * cols, cols), :].T
        return jnp.concatenate([rows * mask for mask in q_masks], axis=0)

    def absorb(s, vp, old=None):
        s = s.reshape(-1, SUBLANES, cols)
        vp = jnp.concatenate([vp] * (cols // LANES), axis=1).reshape(s.shape)
        m = jnp.max(s, axis=0)
        if old is not None:
            m = jnp.maximum(m, old[0])
        e = jnp.exp2((s - m) * scale)
        l = jnp.sum(e, axis=0)
        n = jnp.sum(e * vp, axis=0)
        if old is not None:
            fade = jnp.exp2((old[0] - m) * scale)
            l, n = l + old[1] * fade, n + old[2] * fade
        return m, l, n

    cp_ko.wait()
    cp_vo.wait()
    cp_q.wait()
    def own_part(c, _):
        parts = unpack(k_v[c])
        for i in range(kv):
            kown[:, i * dim:(i + 1) * dim] = parts[i].astype(BF16)
        d = lax.dot_general(v_v[c], probe_t, NT, preferred_element_type=F32)
        split[...] = d
        acc = split[pl.ds(0, clen, stride=kv), :]
        for i in range(1, kv):
            acc = jnp.where(lane_kv == i, split[pl.ds(i, clen, stride=kv), :], acc)
        vpt[...] = acc
        for b in range(blocks):
            n_rows = (b + 1) * tcols
            qt = turn(c, b)
            qt_v[c, b] = qt
            s = jnp.dot(kown[:n_rows, :], qt, preferred_element_type=F32)
            ok = iota((tcols, cols), 0) <= iota((tcols, cols), 1) // heads
            last = jnp.where(ok, s[n_rows - tcols:], NEG)
            s = last if b == 0 else jnp.concatenate([s[:n_rows - tcols], last], axis=0)
            ms[c, b], ls[c, b], ns[c, b] = absorb(s, vpt[:n_rows, :])
        return 0

    lax.fori_loop(0, conts, own_part, 0)

    @pl.when(patient)
    def _():
        share_rest()

    @pl.when(first)
    def _():
        pl.semaphore_wait(column, narrow - 1)
        later(lambda p: signal(everyone, {"wide": p}))

    @pl.when(me_w > 0)
    def _():
        pl.semaphore_wait(everyone, 1)

    others = (wide - 1) * quest
    for cp in scalars:
        cp.wait()
    rows_of = [qrow_ref[slot_ref[c] // ANSWERS] for c in range(conts)]
    drained(vpslot, 1, others).wait_recv()

    def prefix_part(part):
        for c in range(conts):
            for i, x in enumerate(unpack(kslots[part][rows_of[c]])):
                kpre[c, part * half:(part + 1) * half, i * dim:(i + 1) * dim] = x.astype(BF16)
        for c in range(conts):
            keys = pl.ds(part * half, half)
            for b in range(blocks):
                s = jnp.dot(kpre[c, keys], qt_v[c, b], preferred_element_type=F32)
                ms[c, b], ls[c, b], ns[c, b] = absorb(
                    s, vptp[c, keys], (ms[c, b], ls[c, b], ns[c, b])
                )

    for c in range(conts):
        vptp[c] = lax.dot_general(vpslot[rows_of[c]], expand, TN, preferred_element_type=F32)
    drained(kslot_a, 0, others).wait_recv()
    prefix_part(0)
    drained(kslot_b, 4, others).wait_recv()
    prefix_part(1)

    fold = jnp.where(iota((cols, clen), 0) // heads == iota((cols, clen), 1) % tcols, 1.0, 0.0)
    fold = fold.astype(BF16)
    keep = iota((blocks, clen), 1) // tcols == iota((blocks, clen), 0)
    ratios = []
    for c in range(conts):
        m = ms[c]
        fade = jnp.exp2((m - jnp.max(m, axis=1, keepdims=True)) * scale)
        ratios.append(jnp.sum(ns[c] * fade, axis=1) / jnp.sum(ls[c] * fade, axis=1))
    ratio = jnp.concatenate(ratios, axis=0)
    coarse = ratio.astype(BF16)
    fine = (ratio - coarse.astype(F32)).astype(BF16)
    y = jnp.dot(coarse, fold, preferred_element_type=F32)
    y = y + jnp.dot(fine, fold, preferred_element_type=F32)
    y = jnp.where(keep, y.reshape(conts, blocks, clen), 0.0)
    partial = jnp.sum(y, axis=1)
    tslot[me_n] = partial

    tpos = iota((1, clen), 1)
    places = iota((wide, quest * ANSWERS, 1), 0) * (quest * ANSWERS)
    places = places + iota((wide, quest * ANSWERS, 1), 1)
    term = jnp.zeros((wide, quest * ANSWERS, clen), F32)
    for c in range(conts):
        val = jnp.where(tpos < len_ref[c], partial[c:c + 1, :], 0.0)
        place = rows_of[c] * ANSWERS + slot_ref[c] % ANSWERS
        term = jnp.where(places == place, val[None], term)
    cbuf[...] = term

    def hand(i, j):
        to = {"wide": wides[i], "narrow": narrows[j]}
        remote(cbuf.at[wides[i]], cslot.at[me], 2, to).start()

    if total <= 16:
        for j in range(narrow - 1, -1, -1):
            for i in (*far, 0):
                if i or j:
                    hand(i, j)
    else:
        @pl.loop(1, total)
        def _(n):
            p = lax.rem(me + n, total)
            to = {"wide": lax.div(p, narrow), "narrow": lax.rem(p, narrow)}
            remote(cbuf.at[to["wide"]], cslot.at[me], 2, to).start()

    for j in range(1, narrow):
        remote(tslot.at[me_n], tslot.at[me_n], 3, {"narrow": narrows[j]}).start()
    cslot[me] = cbuf[me_w]

    drained(tslot, 3, narrow - 1).wait_recv()
    tok = tslot[0]
    for i in range(1, narrow):
        tok = tok + tslot[i]
    out_ref[0:conts, :] = tok

    drained(cslot, 2, total - 1).wait_recv()
    drained(tslot, 3, narrow - 1).wait_send()
    drained(cslot, 2, total - 1).wait_send()
    for n, buf in ((0, kslot_a), (1, vpslot), (4, kslot_b)):
        drained(buf, n, others).wait_send()
    summed = jnp.sum(jnp.sum(cslot[...], axis=0), axis=1, keepdims=True)
    logps = []
    losses = []
    for r in range(quest):
        score = summed[r * ANSWERS:(r + 1) * ANSWERS]
        top = jnp.max(score, axis=0, keepdims=True)
        norm = jnp.log(jnp.sum(jnp.exp(score - top), axis=0, keepdims=True))
        logp = score - top - norm
        gold = jnp.zeros((1, 1), jnp.int32)
        for g in range(questions):
            gold = jnp.where(me_w * quest + r == qrow_ref[g], gold_ref[g], gold)
        answer = iota((ANSWERS, LANES), 0)
        row = jnp.sum(jnp.where(answer == iota((ANSWERS, LANES), 1), logp, 0.0), axis=0, keepdims=True)
        loss = jnp.sum(jnp.where(answer == gold, -logp, 0.0), axis=0, keepdims=True)
        logps.append(row)
        losses.append(loss)
    for r in range(quest):
        out_ref[conts + r:conts + r + 1, :] = logps[r]
        out_ref[conts + quest + r:conts + quest + r + 1, :] = losses[r]


def hand_out(conts, quest, packed_ref, tok_ref, logp_ref, loss_ref):
    tok_ref[...] = packed_ref[0:conts, :]
    logp_ref[...] = packed_ref[conts:conts + quest, :ANSWERS]
    loss_ref[...] = packed_ref[conts + quest:conts + 2 * quest, :1]


def solution(mesh):
    wide, narrow = mesh.shape["wide"], mesh.shape["narrow"]
    total = wide * narrow

    def per_device(q, k, v, prefix, probe, qrow, slot, length, gold):
        conts, clen, heads, dim = q.shape
        kv = k.shape[2]
        quest, _, pref = prefix.shape[:3]
        questions = qrow.shape[0]
        cols = 2 * LANES // heads * heads
        blocks = clen * heads // cols
        sizes = (wide, narrow, conts, clen, heads, kv, dim, quest, pref, questions)
        vmem = pl.BlockSpec(memory_space=pltpu.VMEM)
        anyw = pl.BlockSpec(memory_space=pl.ANY)
        stat = pltpu.VMEM((conts, blocks, SUBLANES, cols), F32)
        dma = pltpu.SemaphoreType.DMA
        packed = pl.pallas_call(
            functools.partial(kernel, sizes),
            out_shape=pltpu.VMEM((conts + 2 * quest, LANES), F32),
            in_specs=[anyw] * 9,
            out_specs=vmem,
            scratch_shapes=[
                pltpu.SMEM((questions,), jnp.int32),
                pltpu.SMEM((conts,), jnp.int32),
                pltpu.SMEM((conts,), jnp.int32),
                pltpu.SMEM((questions,), jnp.int32),
                pltpu.VMEM((heads, dim), BF16),
                pltpu.VMEM((conts, blocks, kv * dim, cols), BF16),
                pltpu.VMEM((conts, clen * heads, dim), BF16),
                pltpu.VMEM((conts, clen * kv, dim), BF16),
                pltpu.VMEM((conts, clen * kv, dim), BF16),
                pltpu.VMEM((quest, pref * kv, dim), BF16),
                pltpu.VMEM((wide * quest, pref // 2 * kv, dim), BF16),
                pltpu.VMEM((wide * quest, pref // 2 * kv, dim), BF16),
                pltpu.VMEM((wide * quest, heads, pref), BF16),
                pltpu.VMEM((clen * kv, dim), F32),
                pltpu.VMEM((clen, kv * dim), BF16),
                pltpu.VMEM((clen, LANES), F32),
                pltpu.VMEM((conts, pref, kv * dim), BF16),
                pltpu.VMEM((conts, pref, LANES), F32),
                stat, stat, stat,
                pltpu.VMEM((narrow, conts, clen), F32),
                pltpu.VMEM((wide, quest * ANSWERS, clen), F32),
                pltpu.VMEM((total, quest * ANSWERS, clen), F32),
                dma((11,)),
                dma((5,)), dma((5,)),
                pltpu.SemaphoreType.REGULAR((wide,)),
                pltpu.SemaphoreType.REGULAR,
                pltpu.SemaphoreType.REGULAR,
            ],
            compiler_params=pltpu.CompilerParams(collective_id=0, has_side_effects=True),
        )(
            qrow, slot, length, gold,
            q.reshape(conts, clen * heads, dim),
            k.reshape(conts, clen * kv, dim),
            v.reshape(conts, clen * kv, dim),
            prefix.reshape(quest, 2, pref * kv, dim),
            probe,
        )
        tok, logp, loss = pl.pallas_call(
            functools.partial(hand_out, conts, quest),
            out_shape=(
                jax.ShapeDtypeStruct((conts, clen), F32),
                jax.ShapeDtypeStruct((quest, ANSWERS), F32),
                jax.ShapeDtypeStruct((quest, 1), F32),
            ),
            in_specs=[vmem],
            out_specs=(vmem, vmem, vmem),
        )(pltpu.with_memory_space_constraint(packed, pltpu.VMEM))
        return tok, logp, loss.reshape(quest)

    return jax.shard_map(
        per_device,
        mesh=mesh,
        in_specs=(
            P(("groups", "wide"), None, "narrow", None),
            P(("groups", "wide"), None, "narrow", None),
            P(("groups", "wide"), None, "narrow", None),
            P(("groups", "wide"), None, None, "narrow", None),
            P("narrow", None),
            P("groups"),
            P(("groups", "wide")),
            P(("groups", "wide")),
            P("groups"),
        ),
        out_specs=(P(("groups", "wide"), None), P(("groups", "wide"), None), P(("groups", "wide"))),
        check_vma=False,
    )
```

time: 22.1 us -> 19.7 us (0.89)
  Pallas kernels: 21.3 us -> 18.9 us
    pallas_call x1, Pallas kernels: 20.7 us -> 18.3 us  [per_device(): pl.pallas_call(functools.partial(kernel, sizes), out_shape=pltpu.VMEM((co...]
where the time goes in v2:
time: 19.7 us; the launch traced here: 19.6 us
  Pallas kernels  18.9 us (96%)
  between operations  0.64 us (3%)
    pallas_call x1, Pallas kernels, per_device(): pl.pallas_call(functools.partial(kernel, sizes), out_shape=pltpu.VMEM((co...  18.3 us
    pallas_call x1, Pallas kernels, per_device(): pl.pallas_call(functools.partial(hand_out, conts, quest), out_shape=(jax....  0.59 us

profile of v2, /device:TPU:0, one launch (start us, length us, event | category | flops | bytes accessed | tf_op | source)
XLA Modules:
  0.0 19.6 jit_solution(2926118613940365258)
XLA Ops:
  0.6 18.3 %shard_map.112.packed_ref = f32[6,128]{1,0:T(8,128)S(1)} custom-call(s32[4]{0:T(128)} %qrow_hbm.1, s32[4]{0:T(128)} %slot_hbm.1, s32[4]{0:T(128)} %len_hbm.1, s32[4]{0:T(128)} %gold_hbm.1, bf16[4,2048,128]{2,1,0:T(8,128)(2,1)} %bitcast.5, bf16[4,256,128]{2,1,0:T(8,128)(2,1)} %bitcast.6, bf16[4,256,128]{2,1,0:T(8,128)(2,1)} %bitcast.7, ...), custom_call_target="tpu_custom_call" | custom-call | tf_op jit(solution)/shard_map/pallas_call | solution.py:351
  19.0 0.6 %shard_map.113 = (f32[4,128]{1,0:T(4,128)}, f32[1,4]{1,0:T(1,128)}, f32[1,1]{1,0:T(1,128)}) custom-call(f32[6,128]{1,0:T(8,128)S(1)} %shard_map.112.packed_ref), custom_call_target="tpu_custom_call" | custom-call | tf_op jit(solution)/shard_map/pallas_call | solution.py:394
